TPU v7x, 256 devices: a whole 4x4x8 slice. The times are simulated.
256 devices in a mesh: expert: 32 (over x, z_hi, core), tensor: 8 (over y, z_lo).
Axes of the slice: x: 4, y: 4, z: 8 (z_hi: 4, z_lo: 2; z = z_hi * 2 + z_lo), core: 2. Of those that a mesh axis runs over, the one named last changes fastest.
Arguments:
- tokens: bfloat16 [512, 7168], P('expert'), may hold values from -6 to 6
- routes: int32 [512, 8], P('expert'), may hold values from 0 to 31, all different within a row; in each aligned block of 16 rows (0 to 15, 16 to 31, ...) at most 8 rows name the same one
- route_logits: float32 [512, 8], P('expert'), may hold values from -8 to 8
- gate_weight: bfloat16 [32, 7168, 1024], P('expert', 'tensor'), may hold values from -0.0625 to 0.0625
- up_weight: bfloat16 [32, 7168, 1024], P('expert', 'tensor'), may hold values from -0.0625 to 0.0625
- down_weight: bfloat16 [32, 7168, 1024], P('expert', 'tensor'), may hold values from -0.1875 to 0.1875
Outputs:
- mixed: bfloat16 [512, 7168], P('expert', 'tensor')
Inputs may be any that keep to these rules, and one draw needn't show every extreme that they name: `routes`: each row names 8 different experts. In each aligned block of 16 rows (the rows of one index of expert) no expert is named by more than 8 rows, a bound that some block reaches.
All inputs are finite; a program needn't handle non-finite values.
Results may differ from a plain program's by a relative error of at most 0.0066.
Values may be sent and summed in bfloat16 or wider, within the bound.
No kernel may reach another device: no remote copies, remote signals or barrier semaphores. Data moves between devices by JAX's collectives and lax.ppermute only.
A program may use at most 64 MiB of HBM per device.

v0:
```python
import jax
import jax.numpy as jnp
from jax import lax
from jax.sharding import PartitionSpec as P

routed_scale = 2.5


def cut_along(array, dim, peers):
    shape = array.shape
    blocks = array.reshape(*shape[:dim], peers, shape[dim] // peers, *shape[dim + 1 :])
    return jnp.moveaxis(blocks, dim, 0)


def summed_on_arrival(array, axis, dim):
    blocks = cut_along(array, dim, lax.axis_size(axis))
    arrived = lax.all_to_all(blocks, axis, split_axis=0, concat_axis=0, tiled=True)
    return arrived.sum(axis=0)


def sent_together(arrays, axis, dim, along):
    both = jnp.concatenate(arrays, axis=along)
    filled, at, finished = (summed_on_arrival(both, axis, dim), 0, [])
    for a in arrays:
        finished.append(lax.slice_in_dim(filled, at, at + a.shape[along], axis=along))
        at += a.shape[along]
    return tuple(finished)


def copy_for_each(array, axis):
    copies = jnp.broadcast_to(array, (lax.axis_size(axis), *array.shape))
    return lax.all_to_all(copies, axis, split_axis=0, concat_axis=0, tiled=True)


def in_order(blocks, dim):
    blocks = jnp.moveaxis(blocks, 0, dim)
    shape = blocks.shape
    return blocks.reshape(*shape[:dim], shape[dim] * shape[dim + 1], *shape[dim + 2 :])


def gathered_copies(array, axis, dim):
    blocks = copy_for_each(array, axis)
    return in_order(blocks, dim)


def shards(tokens, routes, route_logits, gate_weight, up_weight, down_weight):
    group_count = lax.axis_size("expert")
    shard_count = lax.axis_size("tensor")
    tensor_rank = lax.axis_index("tensor")
    local_tokens, model_width = tokens.shape
    route_count = routes.shape[1]
    local_experts = gate_weight.shape[0]
    expert_count = local_experts * group_count
    capacity = local_tokens // 2
    slot_count = expert_count * capacity
    narrow_width = model_width // shard_count
    scores = jax.nn.sigmoid(route_logits)
    weights = routed_scale * scores / jnp.sum(scores, axis=1, keepdims=True)
    flat_routes = routes.reshape(-1)
    one_hot = (flat_routes[:, None] == jnp.arange(expert_count, dtype=jnp.int32)[None, :]).astype(
        jnp.int32
    )
    earlier = jnp.cumsum(one_hot, axis=0) - one_hot
    position = jnp.sum(earlier * one_hot, axis=1)
    target = flat_routes * capacity + position
    matches = (jnp.arange(slot_count, dtype=jnp.int32)[:, None] == target[None, :]).reshape(
        slot_count, local_tokens, route_count
    )
    selector = jnp.sum(matches.astype(jnp.float32), axis=2).astype(jnp.bfloat16)
    combiner = jnp.sum(jnp.where(matches, weights[None, :, :], 0.0), axis=2).T
    own_columns = lax.dynamic_slice_in_dim(tokens, tensor_rank * narrow_width, narrow_width, 1)
    send_rows = jnp.dot(selector, own_columns, preferred_element_type=jnp.float32).astype(
        jnp.bfloat16
    )
    send_rows = send_rows.reshape(expert_count, capacity, own_columns.shape[1])
    received = lax.all_to_all(send_rows, "expert", split_axis=0, concat_axis=1, tiled=True)
    gate_part = jnp.einsum(
        "erd,edf->erf", received, gate_weight, preferred_element_type=jnp.float32
    )
    up_part = jnp.einsum("erd,edf->erf", received, up_weight, preferred_element_type=jnp.float32)
    gate_value, up_value = sent_together((gate_part, up_part), "tensor", 2, 0)
    hidden_part = (jax.nn.silu(gate_value) * up_value).astype(jnp.bfloat16)
    hidden = gathered_copies(hidden_part, "tensor", 2)
    column_rows = jnp.einsum(
        "erf,edf->erd", hidden, down_weight, preferred_element_type=jnp.float32
    )
    returned = lax.all_to_all(
        column_rows.astype(jnp.bfloat16), "expert", split_axis=1, concat_axis=0, tiled=True
    ).astype(column_rows.dtype)
    mixed = jnp.dot(
        combiner,
        returned.reshape(slot_count, narrow_width),
        precision=lax.Precision.HIGHEST,
        preferred_element_type=jnp.float32,
    )
    return mixed.astype(jnp.bfloat16)


def solution(mesh):
    return jax.shard_map(
        shards,
        mesh=mesh,
        in_specs=(
            P("expert", None),
            P("expert", None),
            P("expert", None),
            P("expert", "tensor", None),
            P("expert", "tensor", None),
            P("expert", "tensor", None),
        ),
        out_specs=P("expert", "tensor"),
        check_vma=False,
    )
```

profile of v0, /device:TPU:1, one launch (start us, length us, event | category | flops | bytes accessed | tf_op | source)
XLA Modules:
  0.0 113.4 jit_solution(8549494154525282923)
XLA Ops:
  0.0 0.9 copy.37
  1.1 0.2 reduce_window_sum.11
  1.5 0.7 fusion.18
  2.2 0.7 multiply_divide_fusion
  3.2 1.8 %fusion.5 = bf16[32,8,896]{2,1,0:T(8,128)(2,1)} fusion(bf16[16,7168]{1,0:T(8,128)(2,1)} %param.6, s32[]{:T(128)S(6)} %select_n.8, bf16[256,16]{0,1:T(8,128)(2,1)S(1)} %get-tuple-element.5), kind=kOutput, calls=%fused_computation.7 | convolution fusion | flops 7569408 | bytes 495620 | tf_op jit(solution)/shard_map/dot_general | solution.py:72
  5.0 12.6 %all-to-all-start = ((bf16[32,8,896]{2,1,0:T(8,128)(2,1)}), bf16[32,8,896]{2,1,0:T(8,128)(2,1)S(1)}, u32[]{:S(2)}, u32[]{:S(2)}) async-start(bf16[32,8,896]{2,1,0:T(8,128)(2,1)} %fusion.5), calls=%async_computation | async-start | bytes 917504 | tf_op jit(solution)/shard_map/all_to_all | solution.py:76
  17.6 3.8 %copy.48 = bf16[1024,896]{1,0:T(8,128)(2,1)} copy(bf16[1024,896]{0,1:T(8,128)(2,1)} %bitcast.55) | data formatting | bytes 3670016 | tf_op jit(solution)/shard_map/erd,edf->erf/dot_general | solution.py:80
  21.5 3.8 %copy.47 = bf16[1024,896]{1,0:T(8,128)(2,1)} copy(bf16[1024,896]{0,1:T(8,128)(2,1)} %bitcast.56) | data formatting | bytes 3670016 | tf_op jit(solution)/shard_map/erd,edf->erf/dot_general | solution.py:77
  25.3 8.8 %all-to-all-done = bf16[32,8,896]{2,1,0:T(8,128)(2,1)S(1)} async-done(((bf16[32,8,896]{2,1,0:T(8,128)(2,1)}), bf16[32,8,896]{2,1,0:T(8,128)(2,1)S(1)}, u32[]{:S(2)}, u32[]{:S(2)}) %all-to-all-start) | async-done | bytes 458784 | tf_op jit(solution)/shard_map/all_to_all | solution.py:76
  34.0 2.4 %convolution_bitcast_fusion = f32[1,256,8,128]{3,1,2,0:T(8,128)S(1)} fusion(bf16[8,128,896]{2,1,0:T(8,128)(2,1)} %bitcast.52, bf16[32,8,896]{2,1,0:T(8,128)(2,1)S(1)} %all-to-all-done), kind=kOutput, calls=%fused_computation.3 | convolution fusion | flops 469762048 | bytes 3342336 | tf_op jit(solution)/shard_map/erd,edf->erf/dot_general | solution.py:80
  36.4 0.8 convolution_bitcast_fusion.1
  37.2 0.2 maximum_bitcast_fusion
  37.4 0.2 copy.42
  37.6 31.8 %all_to_all.28 = f32[8,2,256,128]{3,2,1,0:T(8,128)} all-to-all(f32[8,2,256,128]{3,2,1,0:T(8,128)S(1)} %copy.42), channel_id=1, replica_groups=mesh['expert'=32,'tensor'=8] {'tensor'}, dimensions={0} | all-to-all | bytes 4194304 | tf_op jit(solution)/shard_map/all_to_all | solution.py:17
  69.4 1.7 %reduce_sum.52 = f32[2,256,128]{2,1,0:T(8,128)S(1)} reduce(f32[8,2,256,128]{3,2,1,0:T(8,128)} %all_to_all.28, f32[]{:T(128)} %constant.6.clone.1), dimensions={0}, to_apply=%region_5.6 | reduce | flops 458752 | bytes 2359300 | tf_op jit(solution)/shard_map/reduce_sum | solution.py:18
  71.3 11.6 %all_to_all.29 = bf16[8,1,256,128]{2,3,1,0:T(8,128)(2,1)S(1)} all-to-all(bf16[8,1,256,128]{2,3,1,0:T(8,128)(2,1)S(1)} %broadcast_in_dim.22), channel_id=1, replica_groups=mesh['expert'=32,'tensor'=8] {'tensor'}, dimensions={0} | all-to-all | bytes 1048576 | tf_op jit(solution)/shard_map/all_to_all | solution.py:32
  83.0 0.8 fusion.6
  83.7 0.7 copy.58
  84.5 0.5 broadcast.28
  85.0 3.4 %reduce = bf16[256,896]{1,0:T(8,128)(2,1)S(1)} reduce(bf16[256,1,896]{2,1,0:T(2,128)(2,1)S(1)} %bitcast.53, bf16[]{:T(256)} %broadcast.28), dimensions={1}, to_apply=%bitcast.50.reduce_sub_computation | reduce | bytes 917506
  88.4 0.2 reshape.84
  88.6 23.5 %all_to_all.30 = bf16[32,2,3584]{2,1,0:T(2,128)(2,1)S(1)} all-to-all(bf16[32,2,3584]{2,1,0:T(2,128)(2,1)S(1)} %reshape.84), channel_id=1, replica_groups=mesh['expert'=32,'tensor'=8] {'expert'}, dimensions={0} | all-to-all | bytes 917504 | tf_op jit(solution)/shard_map/all_to_all | solution.py:87
  112.1 0.4 reshape.85
  112.5 0.9 convolution_convert_fusion.1
  (14 shorter events, 0.9 us)
Async XLA Ops:
  0.0 83.0 %copy-start = (bf16[1,896,1024]{2,1,0:T(8,128)(2,1)S(1)}, bf16[1,896,1024]{2,1,0:T(8,128)(2,1)}, u32[]{:S(2)}) copy-start(bf16[1,896,1024]{2,1,0:T(8,128)(2,1)} %param.11) | copy-start | bytes 5505028
  5.0 29.0 %all-to-all-start = ((bf16[32,8,896]{2,1,0:T(8,128)(2,1)}), bf16[32,8,896]{2,1,0:T(8,128)(2,1)S(1)}, u32[]{:S(2)}, u32[]{:S(2)}) async-start(bf16[32,8,896]{2,1,0:T(8,128)(2,1)} %fusion.5), calls=%async_computation | async-start | bytes 917504 | tf_op jit(solution)/shard_map/all_to_all | solution.py:76
  34.0 2.4 %copy-start.1 = (bf16[1024,896]{1,0:T(8,128)(2,1)S(1)}, bf16[1024,896]{1,0:T(8,128)(2,1)}, u32[]{:S(2)}) copy-start(bf16[1024,896]{1,0:T(8,128)(2,1)} %copy.47) | copy-start | bytes 5505028
where the time goes:
time: 114 us; the launch traced here: 113 us
  blocking collectives  67 us (59%)
  starting transfers between devices  12.6 us (11%)
  local copies, waits for them, and re-layouts  10.9 us (10%)
  waiting for transfers between devices  8.79 us (8%)
  other arithmetic  7.38 us (6%)
  matrix products  6.64 us (6%)
    all_to_all x1, blocking collectives, summed_on_arrival(): lax.all_to_all(blocks, axis, split_axis=0, concat_axis=0, tiled=True)  31.8 us
    all_to_all x1, blocking collectives, shards(): lax.all_to_all(column_rows.astype(jnp.bfloat16), 'expert', split_axis=1,...  23.5 us
    all_to_all x1, starting transfers between devices, shards(): lax.all_to_all(send_rows, 'expert', split_axis=0, concat_axis=1, tiled=True)  12.6 us
    all_to_all x1, blocking collectives, copy_for_each(): return lax.all_to_all(copies, axis, split_axis=0, concat_axis=0, tiled=True)  11.6 us
    all_to_all x1, waiting for transfers between devices, shards(): lax.all_to_all(send_rows, 'expert', split_axis=0, concat_axis=1, tiled=True)  8.79 us
    dot_general x1, local copies, waits for them, and re-layouts, shards(): jnp.einsum('erd,edf->erf', received, up_weight, preferred_element_type=jn...  3.84 us
    dot_general x1, local copies, waits for them, and re-layouts, shards(): jnp.einsum('erd,edf->erf', received, gate_weight, preferred_element_type=...  3.8 us
    unnamed x1, other arithmetic  3.41 us
  transfers between devices with their start and end apart: 1, of which 1 were waited for; matrix products, arithmetic and copies ran while one was open for 7% of the time, Pallas kernels for 0%

commit v1 on v0

--- a/solution.py
+++ b/solution.py
@@ -84,8 +84,14 @@
     column_rows = jnp.einsum(
         "erf,edf->erd", hidden, down_weight, preferred_element_type=jnp.float32
     )
-    returned = lax.all_to_all(
-        column_rows.astype(jnp.bfloat16), "expert", split_axis=1, concat_axis=0, tiled=True
+    returned = jnp.concatenate(
+        lax.all_to_all(
+            jnp.stack(jnp.split(column_rows.astype(jnp.bfloat16), lax.axis_size("expert"), axis=1)),
+            "expert",
+            0,
+            0,
+        ),
+        axis=0,
     ).astype(column_rows.dtype)
     mixed = jnp.dot(
         combiner,

time: 114 us -> 109 us (0.956)
  other arithmetic: 7.38 us -> 4.1 us
  local copies, waits for them, and re-layouts: 10.9 us -> 9.28 us
    unnamed x1 -> x0, other arithmetic: 3.41 us -> none
    dot_general x1, matrix products: 0.76 us -> 2.37 us  [shards(): jnp.einsum('erd,edf->erf', received, gate_weight, preferred_element_type=...]
    dot_general x1, matrix products: 2.37 us -> 0.76 us  [shards(): jnp.einsum('erd,edf->erf', received, up_weight, preferred_element_type=jn...]
where the time goes in v1:
time: 109 us; the launch traced here: 108 us
  blocking collectives  66.8 us (61%)
  starting transfers between devices  12.6 us (12%)
  local copies, waits for them, and re-layouts  9.28 us (9%)
  waiting for transfers between devices  8.78 us (8%)
  matrix products  6.65 us (6%)
  other arithmetic  4.1 us (4%)
    all_to_all x1, blocking collectives, summed_on_arrival(): lax.all_to_all(blocks, axis, split_axis=0, concat_axis=0, tiled=True)  32.2 us
    all_to_all x1, blocking collectives, shards(): lax.all_to_all(jnp.stack(jnp.split(column_rows.astype(jnp.bfloat16), lax....  23.4 us
    all_to_all x1, starting transfers between devices, shards(): lax.all_to_all(send_rows, 'expert', split_axis=0, concat_axis=1, tiled=True)  12.6 us
    all_to_all x1, blocking collectives, copy_for_each(): return lax.all_to_all(copies, axis, split_axis=0, concat_axis=0, tiled=True)  11.2 us
    all_to_all x1, waiting for transfers between devices, shards(): lax.all_to_all(send_rows, 'expert', split_axis=0, concat_axis=1, tiled=True)  8.78 us
    dot_general x1, local copies, waits for them, and re-layouts, shards(): jnp.einsum('erd,edf->erf', received, up_weight, preferred_element_type=jn...  3.83 us
    dot_general x1, local copies, waits for them, and re-layouts, shards(): jnp.einsum('erd,edf->erf', received, gate_weight, preferred_element_type=...  3.81 us
    dot_general x1, matrix products, shards(): jnp.einsum('erd,edf->erf', received, gate_weight, preferred_element_type=...  2.37 us
  transfers between devices with their start and end apart: 1, of which 1 were waited for; matrix products, arithmetic and copies ran while one was open for 7% of the time, Pallas kernels for 0%

profile of v1, /device:TPU:1, one launch (start us, length us, event | category | flops | bytes accessed | tf_op | source)
XLA Modules:
  0.0 108.5 jit_solution(7967980085066919876)
XLA Ops:
  0.0 0.8 fusion.17
  0.8 0.7 multiply_divide_fusion
  1.6 0.8 copy.26
  2.4 0.1 eq.30
  2.5 0.1 fusion.13
  2.6 0.2 reduce_window_sum.11
  2.7 0.2 select_reduce_fusion.1
  3.0 0.2 convert_reduce_fusion
  3.2 1.9 %fusion.5 = bf16[32,8,896]{2,1,0:T(8,128)(2,1)} fusion(bf16[16,7168]{1,0:T(8,128)(2,1)} %param.6, s32[]{:T(128)S(6)} %select_n.8, bf16[256,16]{0,1:T(8,128)(2,1)S(1)} %get-tuple-element.5), kind=kOutput, calls=%fused_computation.7 | convolution fusion | flops 7569408 | bytes 495620 | tf_op jit(solution)/shard_map/dot_general | solution.py:72
  5.0 12.6 %all-to-all-start = ((bf16[32,8,896]{2,1,0:T(8,128)(2,1)}), bf16[32,8,896]{2,1,0:T(8,128)(2,1)S(1)}, u32[]{:S(2)}, u32[]{:S(2)}) async-start(bf16[32,8,896]{2,1,0:T(8,128)(2,1)} %fusion.5), calls=%async_computation | async-start | bytes 917504 | tf_op jit(solution)/shard_map/all_to_all | solution.py:76
  17.6 3.8 %copy.35 = bf16[1024,896]{1,0:T(8,128)(2,1)} copy(bf16[1024,896]{0,1:T(8,128)(2,1)} %bitcast.177) | data formatting | bytes 3670016 | tf_op jit(solution)/shard_map/erd,edf->erf/dot_general | solution.py:77
  21.4 3.8 %copy.36 = bf16[1024,896]{1,0:T(8,128)(2,1)} copy(bf16[1024,896]{0,1:T(8,128)(2,1)} %bitcast.178) | data formatting | bytes 3670016 | tf_op jit(solution)/shard_map/erd,edf->erf/dot_general | solution.py:80
  25.3 8.8 %all-to-all-done = bf16[32,8,896]{2,1,0:T(8,128)(2,1)S(1)} async-done(((bf16[32,8,896]{2,1,0:T(8,128)(2,1)}), bf16[32,8,896]{2,1,0:T(8,128)(2,1)S(1)}, u32[]{:S(2)}, u32[]{:S(2)}) %all-to-all-start) | async-done | bytes 458784 | tf_op jit(solution)/shard_map/all_to_all | solution.py:76
  34.0 2.4 %convolution_bitcast_fusion.1 = f32[1,256,8,128]{3,1,2,0:T(8,128)S(1)} fusion(bf16[8,128,896]{2,1,0:T(8,128)(2,1)} %bitcast.176, bf16[32,8,896]{2,1,0:T(8,128)(2,1)S(1)} %all-to-all-done), kind=kOutput, calls=%fused_computation.4 | convolution fusion | flops 469762048 | bytes 3342336 | tf_op jit(solution)/shard_map/erd,edf->erf/dot_general | solution.py:77
  36.4 0.8 convolution_bitcast_fusion
  37.2 0.2 maximum_bitcast_fusion
  37.4 0.2 copy.31
  37.6 32.2 %all_to_all.24 = f32[8,2,256,128]{3,2,1,0:T(8,128)} all-to-all(f32[8,2,256,128]{3,2,1,0:T(8,128)S(1)} %copy.31), channel_id=1, replica_groups=mesh['expert'=32,'tensor'=8] {'tensor'}, dimensions={0} | all-to-all | bytes 4194304 | tf_op jit(solution)/shard_map/all_to_all | solution.py:17
  69.8 1.7 %reduce_sum.52 = f32[2,256,128]{2,1,0:T(8,128)S(1)} reduce(f32[8,2,256,128]{3,2,1,0:T(8,128)} %all_to_all.24, f32[]{:T(128)} %constant.6.clone.1), dimensions={0}, to_apply=%region_5.6 | reduce | flops 458752 | bytes 2359300 | tf_op jit(solution)/shard_map/reduce_sum | solution.py:18
  71.5 0.1 copy.33
  71.7 11.2 %all_to_all.25 = bf16[8,1,256,128]{2,3,1,0:T(8,128)(2,1)S(1)} all-to-all(bf16[8,1,256,128]{2,3,1,0:T(8,128)(2,1)S(1)} %broadcast_in_dim.22), channel_id=1, replica_groups=mesh['expert'=32,'tensor'=8] {'tensor'}, dimensions={0} | all-to-all | bytes 1048576 | tf_op jit(solution)/shard_map/all_to_all | solution.py:32
  82.9 0.8 fusion.6
  84.1 23.4 %all_to_all.26 = bf16[32,1,8,896]{3,2,1,0:T(8,128)(2,1)S(1)} all-to-all(bf16[32,1,8,896]{3,2,1,0:T(8,128)(2,1)S(1)} %constant_dynamic-update-slice_fusion), channel_id=1, replica_groups=mesh['expert'=32,'tensor'=8] {'expert'}, dimensions={0} | all-to-all | bytes 917504 | tf_op jit(solution)/shard_map/all_to_all | solution.py:88
  107.5 0.9 convolution_convert_fusion.1
  (41 shorter events, 0.6 us)
Async XLA Ops:
  0.0 82.9 %copy-start = (bf16[1,896,1024]{2,1,0:T(8,128)(2,1)S(1)}, bf16[1,896,1024]{2,1,0:T(8,128)(2,1)}, u32[]{:S(2)}) copy-start(bf16[1,896,1024]{2,1,0:T(8,128)(2,1)} %param.11) | copy-start | bytes 5505028
  5.0 29.0 %all-to-all-start = ((bf16[32,8,896]{2,1,0:T(8,128)(2,1)}), bf16[32,8,896]{2,1,0:T(8,128)(2,1)S(1)}, u32[]{:S(2)}, u32[]{:S(2)}) async-start(bf16[32,8,896]{2,1,0:T(8,128)(2,1)} %fusion.5), calls=%async_computation | async-start | bytes 917504 | tf_op jit(solution)/shard_map/all_to_all | solution.py:76
  34.0 2.4 %copy-start.1 = (bf16[1024,896]{1,0:T(8,128)(2,1)S(1)}, bf16[1024,896]{1,0:T(8,128)(2,1)}, u32[]{:S(2)}) copy-start(bf16[1024,896]{1,0:T(8,128)(2,1)} %copy.36) | copy-start | bytes 5505028
